TPU v7x, 32 devices: a whole 2x2x4 slice. The times are simulated.
32 devices in a mesh: dp: 8 (over y, x, core), mp: 4 (over z).
Axes of the slice: x: 2, y: 2, z: 4, core: 2. Of those that a mesh axis runs over, the one named last changes fastest.
Arguments:
- hidden_in: bfloat16 [4096, 2048], P('dp'), may hold values from -6 to 6
- cotangent: bfloat16 [4096, 2048], P('dp'), may hold values from -6 to 6
- segments: int32 [8, 512], P('dp'), may hold values from 0 to 5, never falling along the last dimension, each value on 1 to 256 neighbouring positions
- live_counts: int32 [8], P('dp'), may hold values from 128 to 512, as said below
- w_query: bfloat16 [2048, 2048], P('dp', 'mp'), may hold values from -0.125 to 0.125
- w_key: bfloat16 [2048, 2048], P('dp', 'mp'), may hold values from -0.125 to 0.125
- w_value: bfloat16 [2048, 2048], P('dp', 'mp'), may hold values from -0.125 to 0.125
- w_output: bfloat16 [2048, 2048], P('mp', 'dp'), may hold values from -0.125 to 0.125
- w_gate: bfloat16 [2048, 8192], P('dp', 'mp'), may hold values from -0.125 to 0.125
- w_up: bfloat16 [2048, 8192], P('dp', 'mp'), may hold values from -0.125 to 0.125
- w_down: bfloat16 [8192, 2048], P('mp', 'dp'), may hold values from -0.0625 to 0.0625
- query_gain: float32 [2048], P('mp'), may hold values from 0.5 to 1.5
- key_gain: float32 [2048], P('mp'), may hold values from 0.5 to 1.5
- attn_gain: float32 [2048], replicated, may hold values from 0.5 to 1.5
- ffn_gain: float32 [2048], replicated, may hold values from 0.5 to 1.5
Outputs:
- hidden_out: bfloat16 [4096, 2048], P('dp')
- grad_in: float32 [4096, 2048], P('dp')
- grad_query: float32 [2048, 2048], P('dp', 'mp')
- grad_key: float32 [2048, 2048], P('dp', 'mp')
- grad_value: float32 [2048, 2048], P('dp', 'mp')
- grad_output_w: float32 [2048, 2048], P('mp', 'dp')
- grad_gate: float32 [2048, 8192], P('dp', 'mp')
- grad_up: float32 [2048, 8192], P('dp', 'mp')
- grad_down: float32 [8192, 2048], P('mp', 'dp')
- grad_query_gain: float32 [2048], P('mp')
- grad_key_gain: float32 [2048], P('mp')
- grad_attn_gain: float32 [2048], replicated
- grad_ffn_gain: float32 [2048], replicated
Inputs may be any that keep to these rules, and one draw needn't show every extreme that they name: Within the rows of one index of dp, segments never fall; each of the 6 documents has 1 to 256 rows and one has exactly 256. `live_counts`: rows of a block at or after its live count are padding; some index of dp has 512 live rows and some has 128.
All inputs are finite; a program needn't handle non-finite values.
Results may differ from a plain program's by a relative error of at most 0.017.
Values may be sent and summed in bfloat16 or wider, within the bound.
A program may use at most 256 MiB of HBM per device.

v0:
```python
import math
import jax
import jax.numpy as jnp
from jax import lax
from jax.sharding import PartitionSpec as P

HD = 128
EPS = 1e-06
THETA = 500000.0


def doc_positions(seg_row):
    row_count = seg_row.shape[0]
    row_index = jnp.arange(row_count, dtype=jnp.int32)
    change = jnp.concatenate([jnp.ones((1,), dtype=bool), seg_row[1:] != seg_row[:-1]])
    doc_start = lax.cummax(jnp.where(change, row_index, jnp.zeros_like(row_index)), axis=0)
    return (row_index - doc_start).astype(jnp.float32)


def rotary_tables(positions, head_size):
    half_size = head_size // 2
    inv_freq = THETA ** (-(jnp.arange(half_size, dtype=jnp.float32) * (2.0 / head_size)))
    angles = positions[:, None] * inv_freq[None, :]
    return (jnp.cos(angles)[:, None, :], jnp.sin(angles)[:, None, :])


def rotate(values, cos_tab, sin_tab):
    half_size = values.shape[2] // 2
    first_half = values[:, :, :half_size]
    second_half = values[:, :, half_size:]
    return jnp.concatenate(
        [
            first_half * cos_tab - second_half * sin_tab,
            second_half * cos_tab + first_half * sin_tab,
        ],
        axis=2,
    )


def rotate_back(grads, cos_tab, sin_tab):
    half_size = grads.shape[2] // 2
    first_half = grads[:, :, :half_size]
    second_half = grads[:, :, half_size:]
    return jnp.concatenate(
        [
            first_half * cos_tab + second_half * sin_tab,
            second_half * cos_tab - first_half * sin_tab,
        ],
        axis=2,
    )


def block_mask(seg_row, offset, block_rows):
    row_index = jnp.arange(seg_row.shape[0])
    same = seg_row[offset : offset + block_rows, None] == seg_row[None, :]
    return same & (row_index[:, None] >= row_index[None, :])


def block_scores(q_blk, k_bf, allowed, score_scale):
    scores = (
        jnp.einsum("qhe,khe->hqk", q_blk, k_bf, preferred_element_type=jnp.float32) * score_scale
    )
    return jnp.where(allowed[None], scores, jnp.float32(-1e30))


def attend_forward(q_bf, k_bf, v_bf, seg_row, score_scale):
    row_count = q_bf.shape[0]
    block_rows = min(512, row_count)
    allowed = block_mask(seg_row, 0, block_rows)
    scores = block_scores(q_bf, k_bf, allowed, score_scale)
    row_max = jnp.max(scores, axis=2, keepdims=True)
    lse = row_max + jnp.log(jnp.sum(jnp.exp(scores - row_max), axis=2, keepdims=True))
    probs = jnp.exp(scores - lse).astype(jnp.bfloat16)
    outputs = jnp.einsum("hqk,khe->qhe", probs, v_bf, preferred_element_type=jnp.float32)
    lse_parts = [lse]
    return (outputs.astype(jnp.bfloat16), lse_parts)


def attend_backward(q_bf, k_bf, v_bf, o_bf, do_bf, lse_parts, seg_row, score_scale):
    row_count = q_bf.shape[0]
    block_rows = min(512, row_count)
    dq_parts = []
    dk_acc = jnp.zeros(k_bf.shape, jnp.float32)
    dv_acc = jnp.zeros(v_bf.shape, jnp.float32)
    for part_index, offset in enumerate(range(0, row_count, block_rows)):
        allowed = block_mask(seg_row, offset, block_rows)
        scores = block_scores(q_bf, k_bf, allowed, score_scale)
        probs = jnp.exp(scores - lse_parts[part_index])
        probs_bf = probs.astype(jnp.bfloat16)
        dprob = jnp.einsum("qhe,khe->hqk", do_bf, v_bf, preferred_element_type=jnp.float32)
        delta = jnp.transpose(
            jnp.sum(do_bf.astype(jnp.float32) * o_bf.astype(jnp.float32), axis=2)
        )[:, :, None]
        dscore = (probs * (dprob - delta)).astype(jnp.bfloat16)
        dq_parts.append(
            jnp.einsum("hqk,khe->qhe", dscore, k_bf, preferred_element_type=jnp.float32)
            * score_scale
        )
        dk_acc = (
            jnp.einsum("hqk,qhe->khe", dscore, q_bf, preferred_element_type=jnp.float32)
            * score_scale
        )
        dv_acc = jnp.einsum("hqk,qhe->khe", probs_bf, do_bf, preferred_element_type=jnp.float32)
    return (dq_parts[0], dk_acc, dv_acc.astype(jnp.bfloat16))


def norm_back(raw, inv_scale, gained, row_sums, width):
    return inv_scale * gained - raw * inv_scale**3 * (row_sums[:, None] / width)


def on_device(
    hidden_in,
    cotangent,
    segments,
    live_counts,
    w_query,
    w_key,
    w_value,
    w_output,
    w_gate,
    w_up,
    w_down,
    query_gain,
    key_gain,
    attn_gain,
    ffn_gain,
):
    gathered = (
        lax.all_gather(w_query, "dp", axis=0, tiled=True),
        lax.all_gather(w_key, "dp", axis=0, tiled=True),
        lax.all_gather(w_value, "dp", axis=0, tiled=True),
        lax.all_gather(w_output, "dp", axis=1, tiled=True),
        lax.all_gather(w_gate, "dp", axis=0, tiled=True),
        lax.all_gather(w_up, "dp", axis=0, tiled=True),
        lax.all_gather(w_down, "dp", axis=1, tiled=True),
    )
    wq_full, wk_full, wv_full, wo_full, wg_full, wu_full, wd_full = gathered
    seg_row = segments[0]
    live_n = live_counts[0]
    row_count, width = hidden_in.shape
    local_width = wq_full.shape[1]
    heads_here = local_width // HD
    score_scale = 1.0 / math.sqrt(HD)
    live_mask = (jnp.arange(row_count, dtype=jnp.int32) < live_n).astype(jnp.float32)[:, None]
    cos_tab, sin_tab = rotary_tables(doc_positions(seg_row), HD)
    q_proj = jnp.dot(hidden_in, wq_full, preferred_element_type=jnp.float32)
    k_proj = jnp.dot(hidden_in, wk_full, preferred_element_type=jnp.float32)
    v_bf = jnp.dot(hidden_in, wv_full, preferred_element_type=jnp.float32).astype(jnp.bfloat16)
    sq_query, sq_key = lax.psum(
        (jnp.sum(q_proj * q_proj, axis=1), jnp.sum(k_proj * k_proj, axis=1)), "mp"
    )
    inv_q = lax.rsqrt(sq_query[:, None] / width + EPS)
    inv_k = lax.rsqrt(sq_key[:, None] / width + EPS)
    q_rot = rotate(
        (q_proj * inv_q * query_gain).reshape(row_count, heads_here, HD), cos_tab, sin_tab
    ).astype(jnp.bfloat16)
    k_rot = rotate(
        (k_proj * inv_k * key_gain).reshape(row_count, heads_here, HD), cos_tab, sin_tab
    ).astype(jnp.bfloat16)
    v_heads = v_bf.reshape(row_count, heads_here, HD)
    o_bf, lse_parts = attend_forward(q_rot, k_rot, v_heads, seg_row, score_scale)
    o_flat = o_bf.reshape(row_count, local_width)
    attn_raw = lax.psum(jnp.dot(o_flat, wo_full, preferred_element_type=jnp.float32), "mp")
    inv_a = lax.rsqrt(jnp.mean(attn_raw * attn_raw, axis=1, keepdims=True) + EPS)
    h_mid = hidden_in.astype(jnp.float32) + attn_raw * inv_a * attn_gain
    h_bf = h_mid.astype(jnp.bfloat16)
    gate_pre = jnp.dot(h_bf, wg_full, preferred_element_type=jnp.float32)
    up_pre = jnp.dot(h_bf, wu_full, preferred_element_type=jnp.float32)
    act_bf = (jax.nn.silu(gate_pre) * up_pre).astype(jnp.bfloat16)
    ffn_raw = lax.psum(jnp.dot(act_bf, wd_full, preferred_element_type=jnp.float32), "mp")
    inv_f = lax.rsqrt(jnp.mean(ffn_raw * ffn_raw, axis=1, keepdims=True) + EPS)
    hidden_out = (live_mask * (h_mid + ffn_raw * inv_f * ffn_gain)).astype(jnp.bfloat16)
    back_weights = (
        lax.all_gather(w_query, "dp", axis=0, tiled=True),
        lax.all_gather(w_key, "dp", axis=0, tiled=True),
        lax.all_gather(w_value, "dp", axis=0, tiled=True),
        lax.all_gather(w_output, "dp", axis=1, tiled=True),
        lax.all_gather(w_gate, "dp", axis=0, tiled=True),
        lax.all_gather(w_up, "dp", axis=0, tiled=True),
        lax.all_gather(w_down, "dp", axis=1, tiled=True),
    )
    wq_back, wk_back, wv_back, wo_back, wg_back, wu_back, wd_back = back_weights
    dy = live_mask * cotangent.astype(jnp.float32)
    g_ffn_gain = jnp.sum(dy * ffn_raw * inv_f, axis=0)
    gained_f = ffn_gain * dy
    d_ffn = norm_back(ffn_raw, inv_f, gained_f, jnp.sum(gained_f * ffn_raw, axis=1), width).astype(
        jnp.bfloat16
    )
    d_act = jnp.dot(d_ffn, wd_back.T, preferred_element_type=jnp.float32)
    sig = jax.nn.sigmoid(gate_pre)
    d_up = (d_act * gate_pre * sig).astype(jnp.bfloat16)
    d_gate = (d_act * up_pre * sig * (1.0 + gate_pre * (1.0 - sig))).astype(jnp.bfloat16)
    ffn_part = jnp.dot(d_gate, wg_back.T, preferred_element_type=jnp.float32) + jnp.dot(
        d_up, wu_back.T, preferred_element_type=jnp.float32
    )
    dh = dy + lax.psum(ffn_part, "mp")
    g_down = jnp.dot(act_bf.T, d_ffn, preferred_element_type=jnp.float32)
    g_gate = jnp.dot(h_bf.T, d_gate, preferred_element_type=jnp.float32)
    g_up = jnp.dot(h_bf.T, d_up, preferred_element_type=jnp.float32)
    g_attn_gain = jnp.sum(dh * attn_raw * inv_a, axis=0)
    gained_a = attn_gain * dh
    d_attn = norm_back(
        attn_raw, inv_a, gained_a, jnp.sum(gained_a * attn_raw, axis=1), width
    ).astype(jnp.bfloat16)
    d_heads = jnp.dot(d_attn, wo_back.T, preferred_element_type=jnp.float32).astype(jnp.bfloat16)
    g_output = jnp.dot(o_flat.T, d_attn, preferred_element_type=jnp.float32)
    dq_rot, dk_rot, d_val = attend_backward(
        q_rot,
        k_rot,
        v_heads,
        o_bf,
        d_heads.reshape(row_count, heads_here, HD),
        lse_parts,
        seg_row,
        score_scale,
    )
    dq_norm = rotate_back(dq_rot, cos_tab, sin_tab).reshape(row_count, local_width)
    dk_norm = rotate_back(dk_rot, cos_tab, sin_tab).reshape(row_count, local_width)
    g_query_gain = jnp.sum(dq_norm * q_proj * inv_q, axis=0)
    g_key_gain = jnp.sum(dk_norm * k_proj * inv_k, axis=0)
    gained_q = query_gain * dq_norm
    gained_k = key_gain * dk_norm
    sums_query, sums_key = lax.psum(
        (jnp.sum(gained_q * q_proj, axis=1), jnp.sum(gained_k * k_proj, axis=1)), "mp"
    )
    dq_bf = norm_back(q_proj, inv_q, gained_q, sums_query, width).astype(jnp.bfloat16)
    dk_bf = norm_back(k_proj, inv_k, gained_k, sums_key, width).astype(jnp.bfloat16)
    dv_bf = d_val.reshape(row_count, local_width)
    input_part = (
        jnp.dot(dq_bf, wq_back.T, preferred_element_type=jnp.float32)
        + jnp.dot(dk_bf, wk_back.T, preferred_element_type=jnp.float32)
        + jnp.dot(dv_bf, wv_back.T, preferred_element_type=jnp.float32)
    )
    grad_in = dh + lax.psum(input_part.astype(jnp.bfloat16), "mp").astype(jnp.float32)
    g_query = jnp.dot(hidden_in.T, dq_bf, preferred_element_type=jnp.float32)
    g_key = jnp.dot(hidden_in.T, dk_bf, preferred_element_type=jnp.float32)
    g_value = jnp.dot(hidden_in.T, dv_bf, preferred_element_type=jnp.float32)
    owned = (
        lax.psum_scatter(g_query, "dp", scatter_dimension=0, tiled=True),
        lax.psum_scatter(g_key, "dp", scatter_dimension=0, tiled=True),
        lax.psum_scatter(g_value, "dp", scatter_dimension=0, tiled=True),
        lax.psum_scatter(g_output, "dp", scatter_dimension=1, tiled=True),
        lax.psum_scatter(g_gate, "dp", scatter_dimension=0, tiled=True),
        lax.psum_scatter(g_up, "dp", scatter_dimension=0, tiled=True),
        lax.psum_scatter(g_down, "dp", scatter_dimension=1, tiled=True),
    )
    gain_totals = lax.psum((g_query_gain, g_key_gain, g_attn_gain, g_ffn_gain), "dp")
    return (
        hidden_out,
        grad_in,
        owned[0],
        owned[1],
        owned[2],
        owned[3],
        owned[4],
        owned[5],
        owned[6],
        gain_totals[0],
        gain_totals[1],
        gain_totals[2],
        gain_totals[3],
    )


def solution(mesh):
    return jax.shard_map(
        on_device,
        mesh=mesh,
        in_specs=(
            P("dp", None),
            P("dp", None),
            P("dp", None),
            P("dp"),
            P("dp", "mp"),
            P("dp", "mp"),
            P("dp", "mp"),
            P("mp", "dp"),
            P("dp", "mp"),
            P("dp", "mp"),
            P("mp", "dp"),
            P("mp"),
            P("mp"),
            P(),
            P(),
        ),
        out_specs=(
            P("dp", None),
            P("dp", None),
            P("dp", "mp"),
            P("dp", "mp"),
            P("dp", "mp"),
            P("mp", "dp"),
            P("dp", "mp"),
            P("dp", "mp"),
            P("mp", "dp"),
            P("mp"),
            P("mp"),
            P(),
            P(),
        ),
        check_vma=False,
    )
```

profile of v0, /device:TPU:0, one launch (start us, length us, event | category | flops | bytes accessed | tf_op | source)
XLA Modules:
  0.0 1542.0 jit_solution(11089845251164984126)
XLA Ops:
  14.4 26.0 %all-gather.12.cloned.1.call-done = bf16[2048,512]{1,0:T(8,128)(2,1)} async-done(((bf16[256,512]{1,0:T(8,128)(2,1)}), bf16[2048,512]{1,0:T(8,128)(2,1)}) %all-gather.12.cloned.1.call-update) | async-done | bytes 2097168 | tf_op jit(solution)/shard_map/all_gather | solution.py:130
  44.0 26.1 %all-gather.10.cloned.1.call-done = bf16[2048,512]{1,0:T(8,128)(2,1)} async-done(((bf16[256,512]{1,0:T(8,128)(2,1)}), bf16[2048,512]{1,0:T(8,128)(2,1)}) %all-gather.10.cloned.1.call-update) | async-done | bytes 2097168 | tf_op jit(solution)/shard_map/all_gather | solution.py:129
  74.0 11.8 all-reduce.2
  112.2 17.5 %all-gather.14.cloned.1.call-done = bf16[512,2048]{1,0:T(8,128)(2,1)} async-done(((bf16[512,256]{1,0:T(8,128)(2,1)}), bf16[512,2048]{1,0:T(8,128)(2,1)}) %all-gather.14.cloned.1.call-update) | async-done | bytes 2097168 | tf_op jit(solution)/shard_map/all_gather | solution.py:132
  129.7 5.0 fusion.24
  137.1 152.8 %all-reduce.8.cloned.1.call-done = f32[512,2048]{1,0:T(8,128)} async-done(((f32[512,2048]{1,0:T(8,128)}), f32[512,2048]{1,0:T(8,128)}) %all-reduce.8.cloned.1.call-update) | async-done | bytes 4194320 | tf_op jit(solution)/shard_map/psum | solution.py:163
  295.4 49.5 %all-gather.16.cloned.1.call-done = bf16[2048,2048]{1,0:T(8,128)(2,1)} async-done(((bf16[256,2048]{1,0:T(8,128)(2,1)}), bf16[2048,2048]{1,0:T(8,128)(2,1)}) %all-gather.16.cloned.1.call-update) | async-done | bytes 8388624 | tf_op jit(solution)/shard_map/all_gather | solution.py:133
  344.9 10.6 fusion.25
  355.4 45.6 %all-gather.18.cloned.1.call-done = bf16[2048,2048]{1,0:T(8,128)(2,1)} async-done(((bf16[256,2048]{1,0:T(8,128)(2,1)}), bf16[2048,2048]{1,0:T(8,128)(2,1)}) %all-gather.18.cloned.1.call-update) | async-done | bytes 8388624 | tf_op jit(solution)/shard_map/all_gather | solution.py:134
  401.0 12.5 multiply_convert_fusion.4
  413.5 45.3 %all-gather.20.cloned.1.call-done = bf16[2048,2048]{1,0:T(8,128)(2,1)} async-done(((bf16[2048,256]{1,0:T(8,128)(2,1)}), bf16[2048,2048]{1,0:T(8,128)(2,1)}) %all-gather.20.cloned.1.call-update) | async-done | bytes 8388624 | tf_op jit(solution)/shard_map/all_gather | solution.py:135
  458.8 10.5 fusion.26
  470.4 154.0 %all-reduce.10.cloned.1.call-done = f32[512,2048]{1,0:T(8,128)} async-done(((f32[512,2048]{1,0:T(8,128)}), f32[512,2048]{1,0:T(8,128)}) %all-reduce.10.cloned.1.call-update) | async-done | bytes 4194320 | tf_op jit(solution)/shard_map/psum | solution.py:170
  630.8 14.1 multiply_convert_fusion.1
  644.9 7.8 fusion.27
  652.7 9.6 convolution_add_fusion
  662.5 153.9 %all-reduce.12.cloned.1.call-done = f32[512,2048]{1,0:T(8,128)} async-done(((f32[512,2048]{1,0:T(8,128)}), f32[512,2048]{1,0:T(8,128)}) %all-reduce.12.cloned.1.call-update) | async-done | bytes 4194320 | tf_op jit(solution)/shard_map/psum | solution.py:196
  823.5 5.5 subtract_convert_fusion
  852.9 9.6 all-reduce.1
  887.7 13.6 fusion.20
  901.4 12.5 fusion.32
  914.2 12.5 fusion.31
  926.8 24.9 %all-reduce = (f32[512]{0:T(512)}, f32[512]{0:T(512)}, f32[2048]{0:T(1024)}, f32[2048]{0:T(1024)}) all-reduce(f32[512]{0:T(512)S(1)} %get-tuple-element.45, f32[512]{0:T(512)S(1)} %get-tuple-element.43, f32[2048]{0:T(1024)S(1)} %get-tuple-element.39, f32[2048]{0:T(1024)S(1)} %get-tuple-element.41), channel_id=1, replica_groups=mesh['dp'=8,'mp'=4] {'dp'}, use_global_device_ids=true, to_apply=%region_29.30 | all-reduce | flops 5120 | bytes 40960 | tf_op jit(solution)/shard_map/psum | solution.py:247
  951.6 5.6 all-reduce.14.cloned.1.call-done
  957.2 6.1 convert_add_fusion
  963.3 47.3 %reduce-scatter.12.cloned.1.call-done = f32[256,512]{0,1:T(8,128)} async-done(((f32[2048,512]{0,1:T(8,128)}), f32[256,512]{0,1:T(8,128)}) %reduce-scatter.12.cloned.1.call-update) | async-done | bytes 524304 | tf_op jit(solution)/shard_map/reduce_scatter | solution.py:241
  1012.6 52.4 %reduce-scatter.8.cloned.1.call-done = f32[256,512]{0,1:T(8,128)} async-done(((f32[2048,512]{0,1:T(8,128)}), f32[256,512]{0,1:T(8,128)}) %reduce-scatter.8.cloned.1.call-update) | async-done | bytes 524304 | tf_op jit(solution)/shard_map/reduce_scatter | solution.py:239
  1067.1 52.3 %reduce-scatter.10.cloned.1.call-done = f32[256,512]{0,1:T(8,128)} async-done(((f32[2048,512]{0,1:T(8,128)}), f32[256,512]{0,1:T(8,128)}) %reduce-scatter.10.cloned.1.call-update) | async-done | bytes 524304 | tf_op jit(solution)/shard_map/reduce_scatter | solution.py:240
  1121.4 52.9 %reduce-scatter.14.cloned.1.call-done = f32[512,256]{1,0:T(8,128)} async-done(((f32[512,2048]{1,0:T(8,128)}), f32[512,256]{1,0:T(8,128)}) %reduce-scatter.14.cloned.1.call-update) | async-done | bytes 524304 | tf_op jit(solution)/shard_map/reduce_scatter | solution.py:242
  1174.2 120.0 %reduce-scatter.20.cloned.1.call-done = f32[2048,256]{1,0:T(8,128)} async-done(((f32[2048,2048]{1,0:T(8,128)}), f32[2048,256]{1,0:T(8,128)}) %reduce-scatter.20.cloned.1.call-update) | async-done | bytes 2097168 | tf_op jit(solution)/shard_map/reduce_scatter | solution.py:245
  1294.3 120.2 %reduce-scatter.18.cloned.1.call-done = f32[256,2048]{1,0:T(8,128)} async-done(((f32[2048,2048]{1,0:T(8,128)}), f32[256,2048]{1,0:T(8,128)}) %reduce-scatter.18.cloned.1.call-update) | async-done | bytes 2097168 | tf_op jit(solution)/shard_map/reduce_scatter | solution.py:244
  1414.5 120.2 %reduce-scatter.16.cloned.1.call-done = f32[256,2048]{1,0:T(8,128)} async-done(((f32[2048,2048]{1,0:T(8,128)}), f32[256,2048]{1,0:T(8,128)}) %reduce-scatter.16.cloned.1.call-update) | async-done | bytes 2097168 | tf_op jit(solution)/shard_map/reduce_scatter | solution.py:243
  (178 shorter events, 118.0 us)
Async XLA Ops:
  7.2 33.2 %all-gather.12.cloned.1.call-start = ((), (), s32[]{:S(2)}) async-start(), calls=%async_computation.9 | async-start | bytes 2359296 | tf_op jit(solution)/shard_map/all_gather | solution.py:130
  7.9 62.2 %all-gather.10.cloned.1.call-start = ((), (), s32[]{:S(2)}) async-start(), calls=%async_computation.8 | async-start | bytes 2359296 | tf_op jit(solution)/shard_map/all_gather | solution.py:129
  8.7 97.5 %all-gather.8.cloned.1.call-start = ((), (), s32[]{:S(2)}) async-start(), calls=%async_computation.7 | async-start | bytes 2359296 | tf_op jit(solution)/shard_map/all_gather | solution.py:131
  9.4 120.3 %all-gather.14.cloned.1.call-start = ((), (), s32[]{:S(2)}) async-start(), calls=%async_computation.10 | async-start | bytes 2359296 | tf_op jit(solution)/shard_map/all_gather | solution.py:132
  10.0 279.9 %all-reduce.8.cloned.1.call-start = ((), (), s32[]{:S(2)}) async-start(), calls=%async_computation.11 | async-start | bytes 8388608 | tf_op jit(solution)/shard_map/psum | solution.py:163
  14.4 55.7 %copy-start.2 = (bf16[512,2048]{1,0:T(8,128)(2,1)S(1)}, bf16[512,2048]{1,0:T(8,128)(2,1)}, u32[]{:S(2)}) copy-start(bf16[512,2048]{1,0:T(8,128)(2,1)} %param.15) | copy-start | bytes 6291460
  43.9 41.8 %copy-start.35 = (f32[512]{0:T(512)S(1)}, f32[512]{0:T(512)}, u32[]{:S(2)}) copy-start(f32[512]{0:T(512)} %param.27) | copy-start | bytes 6148
  74.0 17.7 %copy-start.34 = (f32[512]{0:T(512)S(1)}, f32[512]{0:T(512)}, u32[]{:S(2)}) copy-start(f32[512]{0:T(512)} %param.26) | copy-start | bytes 6148
  101.7 4.4 copy-start.15
  134.7 157.8 %copy-start.32 = (f32[2048]{0:T(1024)S(1)}, f32[2048]{0:T(1024)}, u32[]{:S(2)}) copy-start(f32[2048]{0:T(1024)} %param.28) | copy-start | bytes 24580
  134.7 210.1 %all-gather.16.cloned.1.call-start = ((), (), s32[]{:S(2)}) async-start(), calls=%async_computation.12 | async-start | bytes 9437184 | tf_op jit(solution)/shard_map/all_gather | solution.py:133
  135.3 265.7 %all-gather.18.cloned.1.call-start = ((), (), s32[]{:S(2)}) async-start(), calls=%async_computation.13 | async-start | bytes 9437184 | tf_op jit(solution)/shard_map/all_gather | solution.py:134
  136.1 322.7 %all-gather.20.cloned.1.call-start = ((), (), s32[]{:S(2)}) async-start(), calls=%async_computation.14 | async-start | bytes 9437184 | tf_op jit(solution)/shard_map/all_gather | solution.py:135
  136.8 487.6 %all-reduce.10.cloned.1.call-start = ((), (), s32[]{:S(2)}) async-start(), calls=%async_computation.15 | async-start | bytes 8388608 | tf_op jit(solution)/shard_map/psum | solution.py:170
  469.3 157.9 %copy-start.33 = (f32[2048]{0:T(1024)S(1)}, f32[2048]{0:T(1024)}, u32[]{:S(2)}) copy-start(f32[2048]{0:T(1024)} %param.29) | copy-start | bytes 24580
  469.3 347.1 %all-reduce.12.cloned.1.call-start = ((), (), s32[]{:S(2)}) async-start(), calls=%async_computation.16 | async-start | bytes 8388608 | tf_op jit(solution)/shard_map/psum | solution.py:196
  644.9 7.8 copy-start.38
  662.3 294.9 %all-reduce.14.cloned.1.call-start = ((), (), s32[]{:S(2)}) async-start(), calls=%async_computation.17 | async-start | bytes 4194304 | tf_op jit(solution)/shard_map/psum | solution.py:234
  816.4 5.2 copy-start.1
  816.4 6.5 copy-start.4
  816.4 7.1 copy-start.5
  823.5 5.5 copy-start.26
  823.5 5.5 copy-start.30
  829.0 5.1 copy-start.10
  872.4 138.1 %reduce-scatter.12.cloned.1.call-start = ((), (), s32[]{:S(2)}) async-start(), calls=%async_computation.20 | async-start | bytes 4718592 | tf_op jit(solution)/shard_map/reduce_scatter | solution.py:241
  875.7 189.3 %reduce-scatter.8.cloned.1.call-start = ((), (), s32[]{:S(2)}) async-start(), calls=%async_computation.18 | async-start | bytes 4718592 | tf_op jit(solution)/shard_map/reduce_scatter | solution.py:239
  879.0 240.3 %reduce-scatter.10.cloned.1.call-start = ((), (), s32[]{:S(2)}) async-start(), calls=%async_computation.19 | async-start | bytes 4718592 | tf_op jit(solution)/shard_map/reduce_scatter | solution.py:240
  882.3 5.4 copy-start.6
  882.3 291.9 %reduce-scatter.14.cloned.1.call-start = ((), (), s32[]{:S(2)}) async-start(), calls=%async_computation.21 | async-start | bytes 4718592 | tf_op jit(solution)/shard_map/reduce_scatter | solution.py:242
  887.4 406.9 %reduce-scatter.20.cloned.1.call-start = ((), (), s32[]{:S(2)}) async-start(), calls=%async_computation.24 | async-start | bytes 18874368 | tf_op jit(solution)/shard_map/reduce_scatter | solution.py:245
  901.3 513.2 %reduce-scatter.18.cloned.1.call-start = ((), (), s32[]{:S(2)}) async-start(), calls=%async_computation.23 | async-start | bytes 18874368 | tf_op jit(solution)/shard_map/reduce_scatter | solution.py:244
  913.9 620.8 %reduce-scatter.16.cloned.1.call-start = ((), (), s32[]{:S(2)}) async-start(), calls=%async_computation.22 | async-start | bytes 18874368 | tf_op jit(solution)/shard_map/reduce_scatter | solution.py:243
  (25 other events, 66.5 us)
Sparse Core Ops, SparseCore 0:
  9.9 30.4 all-gather.11
  42.3 27.7 all-gather.9
  72.0 27.7 all-gather.7
  101.5 28.0 all-gather.13
  134.8 154.9 all-reduce.7
  291.6 53.2 all-gather.15
  346.7 54.2 all-gather.17
  402.9 55.8 all-gather.19
  469.4 154.9 all-reduce.9
  662.4 153.9 all-reduce.11
  872.5 84.6 all-reduce.13
  960.4 50.0 reduce-scatter.11
  1013.9 51.0 reduce-scatter.7
  1068.2 51.0 reduce-scatter.9
  1123.1 51.0 reduce-scatter.13
  1178.2 115.9 reduce-scatter.19
  1298.3 116.1 reduce-scatter.17
  1418.5 116.1 reduce-scatter.15
where the time goes:
time: 1550 us; the launch traced here: 1540 us
  waiting for transfers between devices  1250 us (81%)
  matrix products  149 us (10%)
  other arithmetic  49.8 us (3%)
  blocking collectives  46.3 us (3%)
  local copies, waits for them, and re-layouts  32.1 us (2%)
  between operations  16 us (1%)
    psum x1, waiting for transfers between devices, on_device(): lax.psum(jnp.dot(act_bf, wd_full, preferred_element_type=jnp.float32), 'mp')  154 us
    psum x1, waiting for transfers between devices, on_device(): dh = dy + lax.psum(ffn_part, 'mp')  154 us
    psum x1, waiting for transfers between devices, on_device(): lax.psum(jnp.dot(o_flat, wo_full, preferred_element_type=jnp.float32), 'mp')  153 us
    reduce_scatter x1, waiting for transfers between devices, on_device(): lax.psum_scatter(g_gate, 'dp', scatter_dimension=0, tiled=True)  120 us
    reduce_scatter x1, waiting for transfers between devices, on_device(): lax.psum_scatter(g_up, 'dp', scatter_dimension=0, tiled=True)  120 us
    reduce_scatter x1, waiting for transfers between devices, on_device(): lax.psum_scatter(g_down, 'dp', scatter_dimension=1, tiled=True)  120 us
    reduce_scatter x1, waiting for transfers between devices, on_device(): lax.psum_scatter(g_output, 'dp', scatter_dimension=1, tiled=True)  52.9 us
    reduce_scatter x1, waiting for transfers between devices, on_device(): lax.psum_scatter(g_query, 'dp', scatter_dimension=0, tiled=True)  52.4 us
  transfers between devices with their start and end apart: 18, of which 17 were waited for; matrix products, arithmetic and copies ran while one was open for 8% of the time, Pallas kernels for 0%

commit v1 on v0

--- a/solution.py
+++ b/solution.py
@@ -193,7 +193,7 @@
     ffn_part = jnp.dot(d_gate, wg_back.T, preferred_element_type=jnp.float32) + jnp.dot(
         d_up, wu_back.T, preferred_element_type=jnp.float32
     )
-    dh = dy + lax.psum(ffn_part, "mp")
+    dh = dy + jnp.sum(lax.all_gather(ffn_part, "mp"), axis=0)
     g_down = jnp.dot(act_bf.T, d_ffn, preferred_element_type=jnp.float32)
     g_gate = jnp.dot(h_bf.T, d_gate, preferred_element_type=jnp.float32)
     g_up = jnp.dot(h_bf.T, d_up, preferred_element_type=jnp.float32)

time: 1550 us -> 1690 us (1.090)
  waiting for transfers between devices: 1250 us -> 1380 us
    all_gather x0 -> x1, waiting for transfers between devices: none -> 286 us  [on_device(): dh = dy + jnp.sum(lax.all_gather(ffn_part, 'mp'), axis=0)]
    psum x1 -> x0, waiting for transfers between devices: 154 us -> none  [on_device(): dh = dy + lax.psum(ffn_part, 'mp')]
where the time goes in v1:
time: 1690 us; the launch traced here: 1680 us
  waiting for transfers between devices  1380 us (82%)
  matrix products  150 us (9%)
  other arithmetic  60.1 us (4%)
  blocking collectives  45.2 us (3%)
  local copies, waits for them, and re-layouts  34.2 us (2%)
    all_gather x1, waiting for transfers between devices, on_device(): dh = dy + jnp.sum(lax.all_gather(ffn_part, 'mp'), axis=0)  286 us
    psum x1, waiting for transfers between devices, on_device(): lax.psum(jnp.dot(act_bf, wd_full, preferred_element_type=jnp.float32), 'mp')  154 us
    psum x1, waiting for transfers between devices, on_device(): lax.psum(jnp.dot(o_flat, wo_full, preferred_element_type=jnp.float32), 'mp')  153 us
    reduce_scatter x1, waiting for transfers between devices, on_device(): lax.psum_scatter(g_up, 'dp', scatter_dimension=0, tiled=True)  120 us
    reduce_scatter x1, waiting for transfers between devices, on_device(): lax.psum_scatter(g_gate, 'dp', scatter_dimension=0, tiled=True)  120 us
    reduce_scatter x1, waiting for transfers between devices, on_device(): lax.psum_scatter(g_down, 'dp', scatter_dimension=1, tiled=True)  118 us
    reduce_scatter x1, waiting for transfers between devices, on_device(): lax.psum_scatter(g_output, 'dp', scatter_dimension=1, tiled=True)  54.9 us
    reduce_scatter x1, waiting for transfers between devices, on_device(): lax.psum_scatter(g_query, 'dp', scatter_dimension=0, tiled=True)  52.4 us
  transfers between devices with their start and end apart: 18, of which 17 were waited for; matrix products, arithmetic and copies ran while one was open for 8% of the time, Pallas kernels for 0%

profile of v1, /device:TPU:0, one launch (start us, length us, event | category | flops | bytes accessed | tf_op | source)
XLA Modules:
  0.0 1684.0 jit_solution(10201621891980071070)
XLA Ops:
  14.4 26.0 %all-gather.14.cloned.1.call-done = bf16[2048,512]{1,0:T(8,128)(2,1)} async-done(((bf16[256,512]{1,0:T(8,128)(2,1)}), bf16[2048,512]{1,0:T(8,128)(2,1)}) %all-gather.14.cloned.1.call-update) | async-done | bytes 2097168 | tf_op jit(solution)/shard_map/all_gather | solution.py:130
  44.0 26.1 %all-gather.12.cloned.1.call-done = bf16[2048,512]{1,0:T(8,128)(2,1)} async-done(((bf16[256,512]{1,0:T(8,128)(2,1)}), bf16[2048,512]{1,0:T(8,128)(2,1)}) %all-gather.12.cloned.1.call-update) | async-done | bytes 2097168 | tf_op jit(solution)/shard_map/all_gather | solution.py:129
  74.0 11.8 all-reduce.2
  112.2 17.5 %all-gather.16.cloned.1.call-done = bf16[512,2048]{1,0:T(8,128)(2,1)} async-done(((bf16[512,256]{1,0:T(8,128)(2,1)}), bf16[512,2048]{1,0:T(8,128)(2,1)}) %all-gather.16.cloned.1.call-update) | async-done | bytes 2097168 | tf_op jit(solution)/shard_map/all_gather | solution.py:132
  137.1 152.8 %all-reduce.7.cloned.1.call-done = f32[512,2048]{1,0:T(8,128)} async-done(((f32[512,2048]{1,0:T(8,128)}), f32[512,2048]{1,0:T(8,128)}) %all-reduce.7.cloned.1.call-update) | async-done | bytes 4194320 | tf_op jit(solution)/shard_map/psum | solution.py:163
  295.4 49.5 %all-gather.18.cloned.1.call-done = bf16[2048,2048]{1,0:T(8,128)(2,1)} async-done(((bf16[256,2048]{1,0:T(8,128)(2,1)}), bf16[2048,2048]{1,0:T(8,128)(2,1)}) %all-gather.18.cloned.1.call-update) | async-done | bytes 8388624 | tf_op jit(solution)/shard_map/all_gather | solution.py:133
  344.9 10.6 fusion.25
  355.4 45.6 %all-gather.20.cloned.1.call-done = bf16[2048,2048]{1,0:T(8,128)(2,1)} async-done(((bf16[256,2048]{1,0:T(8,128)(2,1)}), bf16[2048,2048]{1,0:T(8,128)(2,1)}) %all-gather.20.cloned.1.call-update) | async-done | bytes 8388624 | tf_op jit(solution)/shard_map/all_gather | solution.py:134
  401.0 12.5 multiply_convert_fusion.4
  413.5 45.3 %all-gather.22.cloned.1.call-done = bf16[2048,2048]{1,0:T(8,128)(2,1)} async-done(((bf16[2048,256]{1,0:T(8,128)(2,1)}), bf16[2048,2048]{1,0:T(8,128)(2,1)}) %all-gather.22.cloned.1.call-update) | async-done | bytes 8388624 | tf_op jit(solution)/shard_map/all_gather | solution.py:135
  458.8 10.5 fusion.26
  470.4 154.0 %all-reduce.9.cloned.1.call-done = f32[512,2048]{1,0:T(8,128)} async-done(((f32[512,2048]{1,0:T(8,128)}), f32[512,2048]{1,0:T(8,128)}) %all-reduce.9.cloned.1.call-update) | async-done | bytes 4194320 | tf_op jit(solution)/shard_map/psum | solution.py:170
  630.8 14.1 multiply_convert_fusion.1
  645.0 7.8 fusion.27
  652.8 9.6 convolution_add_fusion
  662.4 285.8 %all-gather.24.cloned.1.call-done = f32[2048,2048]{1,0:T(8,128)} async-done(((f32[512,2048]{1,0:T(8,128)}), f32[2048,2048]{1,0:T(8,128)}) %all-gather.24.cloned.1.call-update) | async-done | bytes 16777232 | tf_op jit(solution)/shard_map/all_gather | solution.py:196
  948.2 10.2 reduce_sum.141
  958.4 5.2 multiply_reduce_fusion.1
  965.6 5.5 subtract_convert_fusion
  994.9 8.8 all-reduce.1
  1025.0 13.5 fusion.20
  1038.6 12.6 fusion.32
  1051.5 12.9 fusion.31
  1070.4 24.6 %all-reduce = (f32[512]{0:T(512)}, f32[512]{0:T(512)}, f32[2048]{0:T(1024)}, f32[2048]{0:T(1024)}) all-reduce(f32[512]{0:T(512)S(1)} %get-tuple-element.45, f32[512]{0:T(512)S(1)} %get-tuple-element.43, f32[2048]{0:T(1024)S(1)} %get-tuple-element.39, f32[2048]{0:T(1024)S(1)} %get-tuple-element.41), channel_id=1, replica_groups=mesh['dp'=8,'mp'=4] {'dp'}, use_global_device_ids=true, to_apply=%region_29.30 | all-reduce | flops 5120 | bytes 40960 | tf_op jit(solution)/shard_map/psum | solution.py:247
  1099.1 6.1 convert_add_fusion
  1105.2 47.3 %reduce-scatter.12.cloned.1.call-done = f32[256,512]{0,1:T(8,128)} async-done(((f32[2048,512]{0,1:T(8,128)}), f32[256,512]{0,1:T(8,128)}) %reduce-scatter.12.cloned.1.call-update) | async-done | bytes 524304 | tf_op jit(solution)/shard_map/reduce_scatter | solution.py:241
  1154.5 52.4 %reduce-scatter.8.cloned.1.call-done = f32[256,512]{0,1:T(8,128)} async-done(((f32[2048,512]{0,1:T(8,128)}), f32[256,512]{0,1:T(8,128)}) %reduce-scatter.8.cloned.1.call-update) | async-done | bytes 524304 | tf_op jit(solution)/shard_map/reduce_scatter | solution.py:239
  1209.0 52.3 %reduce-scatter.10.cloned.1.call-done = f32[256,512]{0,1:T(8,128)} async-done(((f32[2048,512]{0,1:T(8,128)}), f32[256,512]{0,1:T(8,128)}) %reduce-scatter.10.cloned.1.call-update) | async-done | bytes 524304 | tf_op jit(solution)/shard_map/reduce_scatter | solution.py:240
  1263.3 118.0 %reduce-scatter.20.cloned.1.call-done = f32[2048,256]{1,0:T(8,128)} async-done(((f32[2048,2048]{1,0:T(8,128)}), f32[2048,256]{1,0:T(8,128)}) %reduce-scatter.20.cloned.1.call-update) | async-done | bytes 2097168 | tf_op jit(solution)/shard_map/reduce_scatter | solution.py:245
  1381.3 120.2 %reduce-scatter.18.cloned.1.call-done = f32[256,2048]{1,0:T(8,128)} async-done(((f32[2048,2048]{1,0:T(8,128)}), f32[256,2048]{1,0:T(8,128)}) %reduce-scatter.18.cloned.1.call-update) | async-done | bytes 2097168 | tf_op jit(solution)/shard_map/reduce_scatter | solution.py:244
  1501.5 120.2 %reduce-scatter.16.cloned.1.call-done = f32[256,2048]{1,0:T(8,128)} async-done(((f32[2048,2048]{1,0:T(8,128)}), f32[256,2048]{1,0:T(8,128)}) %reduce-scatter.16.cloned.1.call-update) | async-done | bytes 2097168 | tf_op jit(solution)/shard_map/reduce_scatter | solution.py:243
  1621.7 54.9 %reduce-scatter.14.cloned.1.call-done = f32[512,256]{1,0:T(8,128)} async-done(((f32[512,2048]{1,0:T(8,128)}), f32[512,256]{1,0:T(8,128)}) %reduce-scatter.14.cloned.1.call-update) | async-done | bytes 524304 | tf_op jit(solution)/shard_map/reduce_scatter | solution.py:242
  (179 shorter events, 123.9 us)
Async XLA Ops:
  7.2 33.2 %all-gather.14.cloned.1.call-start = ((), (), s32[]{:S(2)}) async-start(), calls=%async_computation.9 | async-start | bytes 2359296 | tf_op jit(solution)/shard_map/all_gather | solution.py:130
  7.9 62.2 %all-gather.12.cloned.1.call-start = ((), (), s32[]{:S(2)}) async-start(), calls=%async_computation.8 | async-start | bytes 2359296 | tf_op jit(solution)/shard_map/all_gather | solution.py:129
  8.7 97.5 %all-gather.10.cloned.1.call-start = ((), (), s32[]{:S(2)}) async-start(), calls=%async_computation.7 | async-start | bytes 2359296 | tf_op jit(solution)/shard_map/all_gather | solution.py:131
  9.4 120.3 %all-gather.16.cloned.1.call-start = ((), (), s32[]{:S(2)}) async-start(), calls=%async_computation.10 | async-start | bytes 2359296 | tf_op jit(solution)/shard_map/all_gather | solution.py:132
  10.0 279.9 %all-reduce.7.cloned.1.call-start = ((), (), s32[]{:S(2)}) async-start(), calls=%async_computation.11 | async-start | bytes 8388608 | tf_op jit(solution)/shard_map/psum | solution.py:163
  14.4 55.7 %copy-start.3 = (bf16[512,2048]{1,0:T(8,128)(2,1)S(1)}, bf16[512,2048]{1,0:T(8,128)(2,1)}, u32[]{:S(2)}) copy-start(bf16[512,2048]{1,0:T(8,128)(2,1)} %param.15) | copy-start | bytes 6291460
  43.9 41.9 %copy-start.35 = (f32[512]{0:T(512)S(1)}, f32[512]{0:T(512)}, u32[]{:S(2)}) copy-start(f32[512]{0:T(512)} %param.27) | copy-start | bytes 6148
  74.0 17.7 %copy-start.34 = (f32[512]{0:T(512)S(1)}, f32[512]{0:T(512)}, u32[]{:S(2)}) copy-start(f32[512]{0:T(512)} %param.26) | copy-start | bytes 6148
  101.7 4.4 copy-start.15
  101.7 4.4 copy-start.17
  134.7 157.8 %copy-start.32 = (f32[2048]{0:T(1024)S(1)}, f32[2048]{0:T(1024)}, u32[]{:S(2)}) copy-start(f32[2048]{0:T(1024)} %param.28) | copy-start | bytes 24580
  134.7 210.1 %all-gather.18.cloned.1.call-start = ((), (), s32[]{:S(2)}) async-start(), calls=%async_computation.12 | async-start | bytes 9437184 | tf_op jit(solution)/shard_map/all_gather | solution.py:133
  135.3 265.7 %all-gather.20.cloned.1.call-start = ((), (), s32[]{:S(2)}) async-start(), calls=%async_computation.13 | async-start | bytes 9437184 | tf_op jit(solution)/shard_map/all_gather | solution.py:134
  136.1 322.7 %all-gather.22.cloned.1.call-start = ((), (), s32[]{:S(2)}) async-start(), calls=%async_computation.14 | async-start | bytes 9437184 | tf_op jit(solution)/shard_map/all_gather | solution.py:135
  136.8 487.6 %all-reduce.9.cloned.1.call-start = ((), (), s32[]{:S(2)}) async-start(), calls=%async_computation.15 | async-start | bytes 8388608 | tf_op jit(solution)/shard_map/psum | solution.py:170
  469.3 157.9 %copy-start.33 = (f32[2048]{0:T(1024)S(1)}, f32[2048]{0:T(1024)}, u32[]{:S(2)}) copy-start(f32[2048]{0:T(1024)} %param.29) | copy-start | bytes 24580
  469.3 478.9 %all-gather.24.cloned.1.call-start = ((), (), s32[]{:S(2)}) async-start(), calls=%async_computation.24 | async-start | bytes 20971520 | tf_op jit(solution)/shard_map/all_gather | solution.py:196
  645.0 7.8 copy-start.38
  662.3 436.8 %all-reduce.11.cloned.1.call-start = ((), (), s32[]{:S(2)}) async-start(), calls=%async_computation.16 | async-start | bytes 4194304 | tf_op jit(solution)/shard_map/psum | solution.py:234
  958.4 5.2 copy-start.1
  958.4 6.5 copy-start.2
  958.4 7.1 copy-start.5
  965.6 5.5 copy-start.26
  965.6 5.5 copy-start.30
  971.0 5.1 copy-start.10
  1013.5 139.0 %reduce-scatter.12.cloned.1.call-start = ((), (), s32[]{:S(2)}) async-start(), calls=%async_computation.19 | async-start | bytes 4718592 | tf_op jit(solution)/shard_map/reduce_scatter | solution.py:241
  1016.8 190.1 %reduce-scatter.8.cloned.1.call-start = ((), (), s32[]{:S(2)}) async-start(), calls=%async_computation.17 | async-start | bytes 4718592 | tf_op jit(solution)/shard_map/reduce_scatter | solution.py:239
  1020.1 241.1 %reduce-scatter.10.cloned.1.call-start = ((), (), s32[]{:S(2)}) async-start(), calls=%async_computation.18 | async-start | bytes 4718592 | tf_op jit(solution)/shard_map/reduce_scatter | solution.py:240
  1023.4 357.9 %reduce-scatter.20.cloned.1.call-start = ((), (), s32[]{:S(2)}) async-start(), calls=%async_computation.23 | async-start | bytes 18874368 | tf_op jit(solution)/shard_map/reduce_scatter | solution.py:245
  1038.6 463.0 %reduce-scatter.18.cloned.1.call-start = ((), (), s32[]{:S(2)}) async-start(), calls=%async_computation.22 | async-start | bytes 18874368 | tf_op jit(solution)/shard_map/reduce_scatter | solution.py:244
  1051.2 570.5 %reduce-scatter.16.cloned.1.call-start = ((), (), s32[]{:S(2)}) async-start(), calls=%async_computation.21 | async-start | bytes 18874368 | tf_op jit(solution)/shard_map/reduce_scatter | solution.py:243
  1064.5 612.1 %reduce-scatter.14.cloned.1.call-start = ((), (), s32[]{:S(2)}) async-start(), calls=%async_computation.20 | async-start | bytes 4718592 | tf_op jit(solution)/shard_map/reduce_scatter | solution.py:242
  (25 other events, 61.4 us)
Sparse Core Ops, SparseCore 0:
  9.9 30.4 all-gather.13
  42.3 27.7 all-gather.11
  72.0 27.7 all-gather.9
  101.5 28.0 all-gather.15
  134.8 154.9 all-reduce.6
  291.6 53.2 all-gather.17
  346.7 54.2 all-gather.19
  402.9 55.8 all-gather.21
  469.4 154.9 all-reduce.8
  662.5 285.7 all-gather.23
  1013.6 85.4 all-reduce.10
  1102.3 50.0 reduce-scatter.11
  1155.8 51.0 reduce-scatter.7
  1210.2 51.0 reduce-scatter.9
  1265.3 115.9 reduce-scatter.19
  1385.3 116.2 reduce-scatter.17
  1505.5 116.1 reduce-scatter.15
  1625.5 51.0 reduce-scatter.13
